TPU v7x, 32 devices: a whole 2x2x4 slice. The times are simulated.
32 devices in a mesh: dp: 8 (over z, core), fsdp: 4 (over y, x).
Axes of the slice: x: 2, y: 2, z: 4, core: 2. Of those that a mesh axis runs over, the one named last changes fastest.
Arguments:
- layer_input_tokens: bfloat16 [32768, 768], P(('dp', 'fsdp')), may hold values from -6 to 6
- cotangent: bfloat16 [32768, 768], P(('dp', 'fsdp')), may hold values from -6 to 6
- lengths: int32 [160], P(('dp', 'fsdp')), may hold values from 33 to 512, as said below
- query_key_value_weight: float32 [768, 2304], P(('dp', 'fsdp')), may hold values from -0.21875 to 0.21875
- output_weight: float32 [768, 768], P(('dp', 'fsdp')), may hold values from -0.875 to 0.875
- up_weight: float32 [768, 3072], P(('dp', 'fsdp')), may hold values from -0.21875 to 0.21875
- down_weight: float32 [3072, 768], P(('dp', 'fsdp')), may hold values from -0.109375 to 0.109375
- a_in: float32 [768, 40], P(('dp', 'fsdp')), may hold values from -0.21875 to 0.21875
- a_down: float32 [3072, 8], P(('dp', 'fsdp')), may hold values from -0.109375 to 0.109375
- ln_gains: float32 [2, 768], P(None, ('dp', 'fsdp')), may hold values from 0.5 to 1.5
- ln_biases: float32 [2, 768], P(None, ('dp', 'fsdp')), may hold values from -3 to 3
- adapter_b: float32 [8, 6912], replicated, may hold values from -0.3 to 0.3
- moment_one: float32 [8, 6912], replicated, may hold values from -0.72 to 0.72
- moment_two: float32 [8, 6912], replicated, may hold values from 0.005 to 0.05
Outputs:
- layer_out: bfloat16 [32768, 768], P(('dp', 'fsdp'))
- input_grad: bfloat16 [32768, 768], P(('dp', 'fsdp'))
- b_grad: float32 [8, 6912], replicated
- grad_norm: float32 [], replicated
- moment_one_new: float32 [8, 6912], replicated
- moment_two_new: float32 [8, 6912], replicated
- adapter_b_new: float32 [8, 6912], replicated
Inputs may be any that keep to these rules, and one draw needn't show every extreme that they name: `lengths`: item 5 j + i lies in bucket i of its set; its length is more than half of its bucket and at most the bucket. Some item has exactly 512 valid tokens.
All inputs are finite; a program needn't handle non-finite values.
Results may differ from a plain program's by a relative error of at most 0.012.
The roundings to bfloat16 on the way count: a program that leaves them out, or rounds other values in their place, can miss the bound.
Values may be sent and summed in bfloat16 or wider, within the bound.
A program may use at most 192 MiB of HBM per device.

v0:
```python
import jax
import jax.numpy as jnp
from jax import lax
from jax.sharding import PartitionSpec as P

HEAD = 64
ITEM_LEN = 512
STEP = 10
adapter_scale = 2.0
ln_eps = 1e-05
clip_norm = 256.0
beta_one = 0.9
beta_two = 0.98
learn_rate = 0.02
decay_rate = 0.01


def bucket_plan(full):
    return (
        (0, full, 1, 0),
        (full, full // 2, 1, 1),
        (full * 3 // 2, full // 4, 1, 2),
        (full * 7 // 4, full // 8, 2, 3),
    )


def keep_mask(lengths_set, full):
    parts = []
    for offset, size, count, first in bucket_plan(full):
        positions = jnp.arange(size, dtype=jnp.int32)
        bounds = lengths_set[:, first : first + count]
        mask = (positions[None, None, :] < bounds[:, :, None]).astype(jnp.float32)
        parts.append(mask.reshape(lengths_set.shape[0], count * size))
    return jnp.concatenate(parts, axis=1)


def product_result(left, right):
    return jnp.dot(left, right, preferred_element_type=jnp.float32)


def transposed_product(left, right):
    return lax.dot_general(
        left, right, (((1,), (1,)), ((), ())), preferred_element_type=jnp.float32
    )


def product_tn(left, right):
    return lax.dot_general(
        left, right, (((0,), (0,)), ((), ())), preferred_element_type=jnp.float32
    )


def norm_forward(resid, gain, shift):
    center = resid - jnp.mean(resid, axis=1, keepdims=True)
    variance = jnp.mean(center * center, axis=1, keepdims=True)
    inv_std = lax.rsqrt(variance + ln_eps)
    normed = center * inv_std
    return (normed * gain + shift, normed, inv_std)


def norm_backward(grad_out, normed, inv_std, gain):
    scaled = grad_out * gain
    return inv_std * (
        scaled
        - jnp.mean(scaled, axis=1, keepdims=True)
        - normed * jnp.mean(scaled * normed, axis=1, keepdims=True)
    )


def gelu_exact(values):
    return 0.5 * values * (1.0 + jax.scipy.special.erf(values * 0.7071067811865476))


def gelu_slope(values):
    normal_cdf = 0.5 * (1.0 + jax.scipy.special.erf(values * 0.7071067811865476))
    density = jnp.exp(-0.5 * values * values) * 0.3989422804014327
    return normal_cdf + values * density


def masked_scores(query, key_rows, keep_block):
    scores = (
        jnp.einsum("gqhe,gkhe->ghqk", query, key_rows, preferred_element_type=jnp.float32) * 0.125
    )
    return jnp.where(keep_block[:, None, None, :] > 0.5, scores, -1e30)


def bucket_forward(query, key_rows, value_rows, keep_block):
    scores = masked_scores(query, key_rows, keep_block)
    highest = jnp.max(scores, axis=-1, keepdims=True)
    expo = jnp.exp(scores - highest)
    totals = jnp.sum(expo, axis=-1, keepdims=True)
    probs = (expo / totals).astype(jnp.bfloat16)
    context_rows = jnp.einsum(
        "ghqk,gkhe->gqhe", probs, value_rows, preferred_element_type=jnp.float32
    )
    return (context_rows.astype(jnp.bfloat16), highest + jnp.log(totals))


def bucket_backward(query, key_rows, value_rows, keep_block, log_total, grad_ctx):
    scores = masked_scores(query, key_rows, keep_block)
    probs = jnp.exp(scores - log_total)
    grad_probs = jnp.einsum(
        "gqhe,gkhe->ghqk", grad_ctx, value_rows, preferred_element_type=jnp.float32
    )
    delta = jnp.sum(probs * grad_probs, axis=-1, keepdims=True)
    grad_scores = (probs * (grad_probs - delta)).astype(jnp.bfloat16)
    grad_query = (
        jnp.einsum("ghqk,gkhe->gqhe", grad_scores, key_rows, preferred_element_type=jnp.float32)
        * 0.125
    )
    grad_key = (
        jnp.einsum("ghqk,gqhe->gkhe", grad_scores, query, preferred_element_type=jnp.float32)
        * 0.125
    )
    grad_value = jnp.einsum(
        "ghqk,gqhe->gkhe", probs.astype(jnp.bfloat16), grad_ctx, preferred_element_type=jnp.float32
    )
    return (
        grad_query.astype(jnp.bfloat16),
        grad_key.astype(jnp.bfloat16),
        grad_value.astype(jnp.bfloat16),
    )


def set_forward(operands):
    query, key_rows, value_rows, lens = operands
    heads, size_head = (query.shape[1], query.shape[2])
    keep_set = keep_mask(lens[None, :], ITEM_LEN)[0]
    contexts = []
    totals = []
    for offset, size, count, first in bucket_plan(ITEM_LEN):
        span = count * size
        shape = (count, size, heads, size_head)
        context_rows, log_total = bucket_forward(
            query[offset : offset + span].reshape(shape),
            key_rows[offset : offset + span].reshape(shape),
            value_rows[offset : offset + span].reshape(shape),
            keep_set[offset : offset + span].reshape(count, size),
        )
        contexts.append(context_rows.reshape(span, heads, size_head))
        totals.append(log_total)
    return (jnp.concatenate(contexts, axis=0), tuple(totals))


def set_backward(operands):
    query, key_rows, value_rows, lens, log_totals, grad_ctx = operands
    heads, size_head = (query.shape[1], query.shape[2])
    keep_set = keep_mask(lens[None, :], ITEM_LEN)[0]
    grads_q = []
    grads_k = []
    grads_v = []
    for index, (offset, size, count, first) in enumerate(bucket_plan(ITEM_LEN)):
        span = count * size
        shape = (count, size, heads, size_head)
        grad_q, grad_k, grad_v = bucket_backward(
            query[offset : offset + span].reshape(shape),
            key_rows[offset : offset + span].reshape(shape),
            value_rows[offset : offset + span].reshape(shape),
            keep_set[offset : offset + span].reshape(count, size),
            log_totals[index],
            grad_ctx[offset : offset + span].reshape(shape),
        )
        grads_q.append(grad_q.reshape(span, heads, size_head))
        grads_k.append(grad_k.reshape(span, heads, size_head))
        grads_v.append(grad_v.reshape(span, heads, size_head))
    return (
        jnp.concatenate(grads_q, axis=0),
        jnp.concatenate(grads_k, axis=0),
        jnp.concatenate(grads_v, axis=0),
    )


def adam_update(gradient, grad_norm, moment_old, second_old, weights):
    clipped = gradient * jnp.minimum(1.0, clip_norm / (grad_norm + 1e-06))
    moment_new = beta_one * moment_old + (1.0 - beta_one) * clipped
    second_new = beta_two * second_old + (1.0 - beta_two) * clipped * clipped
    first_hat = moment_new / (1.0 - beta_one**STEP)
    second_hat = second_new / (1.0 - beta_two**STEP)
    weights_new = weights - learn_rate * (
        first_hat / (jnp.sqrt(second_hat) + 1e-08) + decay_rate * weights
    )
    return (moment_new, second_new, weights_new)


def on_device(
    layer_input_tokens,
    cotangent,
    lengths,
    query_key_value_weight,
    output_weight,
    up_weight,
    down_weight,
    a_in,
    a_down,
    ln_gains,
    ln_biases,
    adapter_b,
    moment_one,
    moment_two,
):
    total_rows, width = layer_input_tokens.shape
    span_all = 2 * ITEM_LEN
    sets = total_rows // span_all
    lowrank = adapter_b.shape[0]
    hidden = up_weight.shape[1]
    head_count = width // HEAD
    brain_float_type = jnp.bfloat16
    gathered = (
        lax.all_gather(
            query_key_value_weight.astype(brain_float_type), ("dp", "fsdp"), axis=0, tiled=True
        ),
        lax.all_gather(output_weight.astype(brain_float_type), ("dp", "fsdp"), axis=0, tiled=True),
        lax.all_gather(up_weight.astype(brain_float_type), ("dp", "fsdp"), axis=0, tiled=True),
        lax.all_gather(down_weight.astype(brain_float_type), ("dp", "fsdp"), axis=0, tiled=True),
        lax.all_gather(a_in.astype(brain_float_type), ("dp", "fsdp"), axis=0, tiled=True),
        lax.all_gather(a_down.astype(brain_float_type), ("dp", "fsdp"), axis=0, tiled=True),
        lax.all_gather(ln_gains.astype(brain_float_type), ("dp", "fsdp"), axis=1, tiled=True),
        lax.all_gather(ln_biases.astype(brain_float_type), ("dp", "fsdp"), axis=1, tiled=True),
    )
    (
        projection_weight_gradient,
        output_weight_gradient,
        up_weight_gradient,
        down_weight_gradient,
        g_ain,
        g_adown,
        g_gain,
        g_bias,
    ) = gathered
    gain_full = g_gain.astype(jnp.float32)
    bias_full = g_bias.astype(jnp.float32)
    lengths_set = lengths.reshape(sets, 5)
    keep = keep_mask(lengths_set, ITEM_LEN)
    keep_rows = keep.reshape(-1, 1)
    b_low = adapter_b.astype(brain_float_type)
    query_adapter_matrix = b_low[:, :width]
    key_adapter_matrix = b_low[:, width : 2 * width]
    value_adapter_matrix = b_low[:, 2 * width : 3 * width]
    attention_adapter_bias = b_low[:, 3 * width : 4 * width]
    upper_adapter_matrix = b_low[:, 4 * width : 4 * width + hidden]
    lower_adapter_matrix = b_low[:, 4 * width + hidden :]
    projection_down_matrix = product_result(layer_input_tokens, g_ain[:, : 3 * lowrank]).astype(
        brain_float_type
    )
    adapter_projection_delta = jnp.concatenate(
        [
            product_result(projection_down_matrix[:, :lowrank], query_adapter_matrix),
            product_result(projection_down_matrix[:, lowrank : 2 * lowrank], key_adapter_matrix),
            product_result(projection_down_matrix[:, 2 * lowrank :], value_adapter_matrix),
        ],
        axis=1,
    )
    query_key_value = (
        product_result(layer_input_tokens, projection_weight_gradient)
        + adapter_scale * adapter_projection_delta
    ).astype(brain_float_type)
    qkv_heads = query_key_value.reshape(sets, span_all, 3, head_count, HEAD)
    query = qkv_heads[:, :, 0]
    key_rows = qkv_heads[:, :, 1]
    value_rows = qkv_heads[:, :, 2]
    context_rows, log_totals = lax.map(set_forward, (query, key_rows, value_rows, lengths_set))
    context_token_rows = context_rows.reshape(sets * span_all, width)
    attention_down_matrix = product_result(
        context_token_rows, g_ain[:, 3 * lowrank : 4 * lowrank]
    ).astype(brain_float_type)
    attention_output = product_result(
        context_token_rows, output_weight_gradient
    ) + adapter_scale * product_result(attention_down_matrix, attention_adapter_bias)
    hidden_one, normed_one, inv_one = norm_forward(
        layer_input_tokens.astype(jnp.float32) + attention_output, gain_full[0], bias_full[0]
    )
    hidden_lower_rows = hidden_one.astype(brain_float_type)
    upper_down_matrix = product_result(hidden_lower_rows, g_ain[:, 4 * lowrank :]).astype(
        brain_float_type
    )
    upper_rows = product_result(
        hidden_lower_rows, up_weight_gradient
    ) + adapter_scale * product_result(upper_down_matrix, upper_adapter_matrix)
    active_rows = gelu_exact(upper_rows).astype(brain_float_type)
    lower_down_matrix = product_result(active_rows, g_adown).astype(brain_float_type)
    feedforward_output = product_result(
        active_rows, down_weight_gradient
    ) + adapter_scale * product_result(lower_down_matrix, lower_adapter_matrix)
    output, normed_two, inv_two = norm_forward(
        hidden_one + feedforward_output, gain_full[1], bias_full[1]
    )
    layer_out = (output * keep_rows).astype(brain_float_type)
    again = (
        lax.all_gather(
            query_key_value_weight.astype(brain_float_type), ("dp", "fsdp"), axis=0, tiled=True
        ),
        lax.all_gather(output_weight.astype(brain_float_type), ("dp", "fsdp"), axis=0, tiled=True),
        lax.all_gather(up_weight.astype(brain_float_type), ("dp", "fsdp"), axis=0, tiled=True),
        lax.all_gather(down_weight.astype(brain_float_type), ("dp", "fsdp"), axis=0, tiled=True),
        lax.all_gather(a_in.astype(brain_float_type), ("dp", "fsdp"), axis=0, tiled=True),
        lax.all_gather(a_down.astype(brain_float_type), ("dp", "fsdp"), axis=0, tiled=True),
        lax.all_gather(ln_gains.astype(brain_float_type), ("dp", "fsdp"), axis=1, tiled=True),
        lax.all_gather(ln_biases.astype(brain_float_type), ("dp", "fsdp"), axis=1, tiled=True),
    )
    (
        projection_weight_gradient,
        output_weight_gradient,
        up_weight_gradient,
        down_weight_gradient,
        g_ain,
        g_adown,
        g_gain,
        g_bias,
    ) = again
    gain_full = g_gain.astype(jnp.float32)
    grad_out = cotangent.astype(jnp.float32) * keep_rows
    grad_two = norm_backward(grad_out, normed_two, inv_two, gain_full[1])
    feedforward_gradient = grad_two.astype(brain_float_type)
    lower_down_gradient = (
        adapter_scale * transposed_product(feedforward_gradient, lower_adapter_matrix)
    ).astype(brain_float_type)
    grad_active = transposed_product(
        feedforward_gradient, down_weight_gradient
    ) + transposed_product(lower_down_gradient, g_adown)
    upper_output_gradient = (grad_active * gelu_slope(upper_rows)).astype(brain_float_type)
    upper_down_gradient = (
        adapter_scale * transposed_product(upper_output_gradient, upper_adapter_matrix)
    ).astype(brain_float_type)
    grad_hidden = (
        grad_two
        + transposed_product(upper_output_gradient, up_weight_gradient)
        + transposed_product(upper_down_gradient, g_ain[:, 4 * lowrank :])
    )
    grad_one = norm_backward(grad_hidden, normed_one, inv_one, gain_full[0])
    attention_gradient = grad_one.astype(brain_float_type)
    attention_down_gradient = (
        adapter_scale * transposed_product(attention_gradient, attention_adapter_bias)
    ).astype(brain_float_type)
    grad_ctx = (
        transposed_product(attention_gradient, output_weight_gradient)
        + transposed_product(attention_down_gradient, g_ain[:, 3 * lowrank : 4 * lowrank])
    ).astype(brain_float_type)
    grad_q, grad_k, grad_v = lax.map(
        set_backward,
        (
            query,
            key_rows,
            value_rows,
            lengths_set,
            log_totals,
            grad_ctx.reshape(sets, span_all, head_count, HEAD),
        ),
    )
    grad_qkv = jnp.stack([grad_q, grad_k, grad_v], axis=2).reshape(sets * span_all, 3 * width)
    grad_uqkv = (
        adapter_scale
        * jnp.concatenate(
            [
                transposed_product(grad_qkv[:, :width], query_adapter_matrix),
                transposed_product(grad_qkv[:, width : 2 * width], key_adapter_matrix),
                transposed_product(grad_qkv[:, 2 * width :], value_adapter_matrix),
            ],
            axis=1,
        )
    ).astype(brain_float_type)
    input_grad = (
        grad_one
        + transposed_product(grad_qkv, projection_weight_gradient)
        + transposed_product(grad_uqkv, g_ain[:, : 3 * lowrank])
    ).astype(brain_float_type)
    local_gradient = adapter_scale * jnp.concatenate(
        [
            product_tn(projection_down_matrix[:, :lowrank], grad_qkv[:, :width]),
            product_tn(
                projection_down_matrix[:, lowrank : 2 * lowrank], grad_qkv[:, width : 2 * width]
            ),
            product_tn(projection_down_matrix[:, 2 * lowrank :], grad_qkv[:, 2 * width :]),
            product_tn(attention_down_matrix, attention_gradient),
            product_tn(upper_down_matrix, upper_output_gradient),
            product_tn(lower_down_matrix, feedforward_gradient),
        ],
        axis=1,
    )
    b_grad = lax.psum(local_gradient, ("dp", "fsdp"))
    grad_norm = jnp.sqrt(jnp.sum(b_grad * b_grad))
    moment_new, second_new, adapter_new = adam_update(
        b_grad, grad_norm, moment_one, moment_two, adapter_b
    )
    return (layer_out, input_grad, b_grad, grad_norm, moment_new, second_new, adapter_new)


def solution(mesh):
    placed = (
        P(("dp", "fsdp"), None),
        P(("dp", "fsdp"), None),
        P(("dp", "fsdp")),
        P(("dp", "fsdp"), None),
        P(("dp", "fsdp"), None),
        P(("dp", "fsdp"), None),
        P(("dp", "fsdp"), None),
        P(("dp", "fsdp"), None),
        P(("dp", "fsdp"), None),
        P(None, ("dp", "fsdp")),
        P(None, ("dp", "fsdp")),
        P(),
        P(),
        P(),
    )
    return jax.shard_map(
        on_device,
        mesh=mesh,
        in_specs=placed,
        out_specs=(P(("dp", "fsdp"), None), P(("dp", "fsdp"), None), P(), P(), P(), P(), P()),
        check_vma=False,
    )
```

profile of v0, /device:TPU:8, one launch (start us, length us, event | category | flops | bytes accessed | tf_op | source)
XLA Modules:
  0.0 654.7 jit_solution(7428954899423333268)
XLA Ops:
  7.2 1.7 convert_element_type.392
  10.6 1.6 convert_element_type.423
  12.3 1.6 convert_element_type.426
  22.8 57.2 %all_gather.32 = bf16[768,40]{1,0:T(8,128)(2,1)S(1)} all-gather(bf16[24,40]{1,0:T(8,128)(2,1)S(1)} %convert_element_type.393), channel_id=1, replica_groups=mesh['dp'=8,'fsdp'=4] {'dp','fsdp'}, dimensions={0}, use_global_device_ids=true | all-gather | bytes 63360 | tf_op jit(solution)/shard_map/all_gather | solution.py:215
  80.0 1.6 copy.149
  82.1 2.3 fusion.119
  84.4 2.4 fusion.122
  86.8 2.3 fusion.125
  89.9 64.0 %all-gather.1 = bf16[32,24,2]{1,2,0:T(2,128)(2,1)S(1)} all-gather(bf16[1,24,2]{1,2,0:T(2,128)(2,1)S(1)} %convert_bitcast_fusion.1), channel_id=1, replica_groups=mesh['dp'=8,'fsdp'=4] {'dp','fsdp'}, dimensions={0}, use_global_device_ids=true | all-gather | bytes 3168 | tf_op jit(solution)/shard_map/all_gather | solution.py:218
  154.0 66.0 %all-gather = bf16[32,24,2]{1,2,0:T(2,128)(2,1)S(1)} all-gather(bf16[1,24,2]{1,2,0:T(2,128)(2,1)S(1)} %convert_bitcast_fusion.2), channel_id=1, replica_groups=mesh['dp'=8,'fsdp'=4] {'dp','fsdp'}, dimensions={0}, use_global_device_ids=true | all-gather | bytes 3168 | tf_op jit(solution)/shard_map/all_gather | solution.py:217
  221.7 63.5 %all-gather.2 = bf16[32,96,8]{1,2,0:T(8,128)(2,1)S(1)} all-gather(bf16[1,96,8]{1,2,0:T(8,128)(2,1)S(1)} %convert_bitcast_fusion), channel_id=1, replica_groups=mesh['dp'=8,'fsdp'=4] {'dp','fsdp'}, dimensions={0}, use_global_device_ids=true | all-gather | bytes 50688 | tf_op jit(solution)/shard_map/all_gather | solution.py:216
  285.9 1.6 copy.167
  288.1 8.8 %fusion.9 = bf16[1024,2304]{1,0:T(8,128)(2,1)} fusion(f32[1024,768]{1,0:T(8,128)} %fusion.119, f32[1024,768]{1,0:T(8,128)} %fusion.122, f32[1024,768]{1,0:T(8,128)} %fusion.125, bf16[1024,768]{1,0:T(8,128)(2,1)S(1)} %copy-done.17, bf16[768,2304]{1,0:T(8,128)(2,1)} %all-gather.8.cloned.1.call-done), kind=kOutput, calls=%fused_computation.20 | convolution fusion | flops 3635675136 | bytes 19267584 | tf_op jit(solution)/shard_map/dot_general | solution.py:38
  297.0 6.6 %copy.153 = bf16[1024,2304]{0,1:T(8,128)(2,1)} copy(bf16[1024,2304]{1,0:T(8,128)(2,1)} %fusion.9) | data formatting | bytes 9437184 | tf_op jit(solution)/shard_map/convert_element_type | solution.py:256
  312.3 1.9 fusion.156
  314.2 5.1 fusion.157
  319.8 2.0 fusion.47
  321.8 2.0 copy-done.64
  323.7 1.8 fusion.6
  325.5 4.0 fusion.25
  330.0 2.8 fusion.99
  338.4 7.5 %fusion.162 = f32[1024,3072]{1,0:T(8,128)S(1)} fusion(bf16[1024,768]{0,1:T(8,128)(2,1)} %copy-done.8, bf16[768,3072]{1,0:T(8,128)(2,1)} %all-gather.12.cloned.1.call-done), kind=kOutput, calls=%fused_computation.253 | convolution fusion | flops 4831838208 | bytes 18874368 | tf_op jit(solution)/shard_map/dot_general | solution.py:38
  345.9 7.2 %multiply_convert_fusion.1 = (bf16[1024,3072]{1,0:T(8,128)(2,1)S(1)}, f32[1024,3072]{1,0:T(8,128)}) fusion(f32[1024,3072]{1,0:T(8,128)S(1)} %fusion.162, bf16[1024,8]{0,1:T(8,128)(2,1)S(1)} %convolution_convert_fusion.6, bf16[8,6912]{1,0:T(8,128)(2,1)S(1)} %convert_element_type.395), kind=kOutput, calls=%fused_computation.10 | convolution fusion | flops 72351744 | bytes 31522816 | tf_op jit(solution)/shard_map/dot_general | solution.py:38
  353.1 2.7 copy-done.6
  355.8 1.7 convolution_convert_fusion.5
  357.5 8.8 %fusion.163 = f32[1024,768]{0,1:T(8,128)S(1)} fusion(bf16[1024,3072]{1,0:T(8,128)(2,1)} %copy-done.6, bf16[3072,768]{1,0:T(8,128)(2,1)} %all-gather.14.cloned.1.call-done), kind=kOutput, calls=%fused_computation.254 | convolution fusion | flops 4831838208 | bytes 14155776 | tf_op jit(solution)/shard_map/dot_general | solution.py:38
  367.9 2.1 copy-done.5
  370.9 2.6 fusion.108
  373.5 8.0 %fusion.164 = f32[1024,3072]{1,0:T(8,128)} fusion(bf16[1024,768]{0,1:T(8,128)(2,1)S(1)} %get-tuple-element.118, bf16[3072,768]{1,0:T(8,128)(2,1)S(1)} %bitcast.280), kind=kOutput, calls=%fused_computation.255 | convolution fusion | flops 4831838208 | bytes 18874368 | tf_op jit(solution)/shard_map/dot_general | solution.py:42
  381.5 13.7 %fusion.5 = bf16[1024,3072]{1,0:T(8,128)(2,1)} fusion(f32[1024,3072]{1,0:T(8,128)} %get-tuple-element.136, f32[1024,3072]{1,0:T(8,128)} %fusion.164, bf16[3072,8]{0,1:T(8,128)(2,1)S(1)} %copy-done.47, bf16[1024,768]{0,1:T(8,128)(2,1)} %copy-done.18, bf16[8,6912]{1,0:T(8,128)(2,1)S(1)} %convert_element_type.395), kind=kOutput, calls=%fused_computation.6 | convolution fusion | flops 97533952 | bytes 33091584 | tf_op jit(solution)/shard_map/dot_general | solution.py:42
  395.2 10.0 %fusion.165 = f32[1024,768]{0,1:T(8,128)} fusion(bf16[1024,3072]{1,0:T(8,128)(2,1)} %fusion.5, bf16[768,3072]{1,0:T(8,128)(2,1)} %all-gather.12.cloned.1.call-done), kind=kOutput, calls=%fused_computation.256 | convolution fusion | flops 4831838208 | bytes 14155776 | tf_op jit(solution)/shard_map/dot_general | solution.py:42
  405.2 10.2 %fusion.149 = (f32[1024]{0:T(1024)S(1)}, f32[1024]{0:T(1024)S(1)}, f32[1024,768]{0,1:T(8,128)}) fusion(f32[1024]{0:T(1024)S(1)} %copy-done.53, f32[1024,768]{0,1:T(8,128)S(1)} %get-tuple-element.134, f32[1024]{0:T(1024)S(1)} %broadcast_multiply_fusion.6, f32[768]{0:T(1024)S(1)} %copy-done.62, bf16[768,40]{1,0:T(8,128)(2,1)S(1)} %all_gather.32, ...), kind=kOutput, calls=%fused_computation.243 | convolution fusion | flops 76298240 | bytes 20738048 | tf_op jit(solution)/shard_map/dot_general | solution.py:42
  415.5 2.8 fusion.84
  419.5 3.0 fusion.166
  422.5 4.4 add_convert_fusion.1
  426.9 1.8 slice.306
  428.7 1.7 fusion.152
  430.4 2.1 slice.305
  432.5 1.9 reshape.739
  434.4 1.7 fusion.54
  436.1 1.7 multiply_reduce_fusion.6
  442.8 2.0 fusion.64
  444.8 1.9 fusion.65
  448.1 1.9 multiply_reduce_fusion.1
  450.7 2.6 fusion.55
  453.3 2.2 fusion.56
  455.5 3.2 fusion.38
  458.7 7.1 %multiply_reduce_fusion = (f32[12,512]{1,0:T(8,128)S(1)}, f32[12,512,512]{1,2,0:T(8,128)}) fusion(f32[12,512,512]{1,2,0:T(8,128)S(1)} %bitcast.240, f32[12,512]{1,0:T(8,128)S(1)} %copy-done.39, bf16[512,12,64]{0,2,1:T(8,128)(2,1)S(1)} %bitcast.267, bf16[1,1024,3,12,64]{1,4,3,2,0:T(8,128)(2,1)} %bitcast.254), kind=kOutput, calls=%fused_computation.8 | convolution fusion | flops 412084224 | bytes 26787840 | tf_op jit(solution)/shard_map/while/body/eval_jaxpr/gqhe,gkhe->ghqk/dot_general | solution.py:102
  465.8 6.8 %multiply_convert_fusion = bf16[12,512,512]{1,2,0:T(8,128)(2,1)S(1)} fusion(f32[12,512,512]{1,2,0:T(8,128)} %get-tuple-element.147, f32[12,512,512]{1,2,0:T(8,128)S(1)} %bitcast.240, f32[12,512]{1,0:T(8,128)S(1)} %get-tuple-element.146, f32[12,512]{1,0:T(8,128)S(1)} %copy-done.39), kind=kLoop, calls=%fused_computation.7 | loop fusion | flops 12582912 | bytes 31506432 | tf_op jit(solution)/shard_map/while/body/eval_jaxpr/convert_element_type | solution.py:106
  472.6 4.0 fusion.43
  476.7 3.1 fusion.42
  481.0 1.9 reshape.748
  482.9 1.9 copy.176
  484.8 1.9 reshape.740
  486.7 1.9 copy.183
  488.6 1.9 reshape.744
  490.6 1.7 maximum_bitcast_fusion.2
  494.9 2.6 fusion.32
  503.4 6.9 %fusion.167 = f32[1024,768]{0,1:T(8,128)S(1)} fusion(bf16[768,2304]{1,0:T(8,128)(2,1)} %all-gather.8.cloned.1.call-done, bf16[1024,2304]{0,1:T(8,128)(2,1)} %bitcast.265), kind=kOutput, calls=%fused_computation.258 | convolution fusion | flops 3623878656 | bytes 11403264 | tf_op jit(solution)/shard_map/dot_general | solution.py:42
  510.4 2.3 add_convert_fusion
  512.7 2.7 copy.192
  517.0 123.7 %all-reduce.2.cloned.1.call-done = f32[8,6912]{1,0:T(8,128)} async-done(((f32[8,6912]{1,0:T(8,128)}), f32[8,6912]{1,0:T(8,128)}) %all-reduce.2.cloned.1.call-update) | async-done | bytes 221200 | tf_op jit(solution)/shard_map/psum | solution.py:379
  643.1 1.9 multiply_subtract_fusion
  644.9 1.6 copy.241
  (284 shorter events, 53.2 us)
Async XLA Ops:
  7.2 72.8 %copy-start.17 = (bf16[1024,768]{1,0:T(8,128)(2,1)S(1)}, bf16[1024,768]{1,0:T(8,128)(2,1)}, u32[]{:S(2)}) copy-start(bf16[1024,768]{1,0:T(8,128)(2,1)} %param.14) | copy-start | bytes 4718596
  7.2 281.0 %all-gather.8.cloned.1.call-start = ((), (), s32[]{:S(2)}) async-start(), calls=%async_computation | async-start | bytes 3649536 | tf_op jit(solution)/shard_map/all_gather | solution.py:209
  8.9 321.0 %all-gather.10.cloned.1.call-start = ((), (), s32[]{:S(2)}) async-start(), calls=%async_computation.1 | async-start | bytes 1216512 | tf_op jit(solution)/shard_map/all_gather | solution.py:212
  10.5 327.8 %all-gather.12.cloned.1.call-start = ((), (), s32[]{:S(2)}) async-start(), calls=%async_computation.2 | async-start | bytes 4866048 | tf_op jit(solution)/shard_map/all_gather | solution.py:213
  12.2 345.3 %all-gather.14.cloned.1.call-start = ((), (), s32[]{:S(2)}) async-start(), calls=%async_computation.3 | async-start | bytes 4866048 | tf_op jit(solution)/shard_map/all_gather | solution.py:214
  13.9 626.8 %all-reduce.2.cloned.1.call-start = ((), (), s32[]{:S(2)}) async-start(), calls=%async_computation.4 | async-start | bytes 442368 | tf_op jit(solution)/shard_map/psum | solution.py:379
  22.8 399.7 %copy-start.38 = (bf16[8,6912]{1,0:T(8,128)(2,1)}, bf16[8,6912]{1,0:T(8,128)(2,1)S(1)}, u32[]{:S(2)}) copy-start(bf16[8,6912]{1,0:T(8,128)(2,1)S(1)} %convert_element_type.395) | copy-start | bytes 331780
  82.1 4.7 copy-start.40
  84.4 5.4 copy-start.81
  84.4 5.4 copy-start.82
  84.4 5.5 copy-start.77
  84.4 201.5 %copy-start.26 = (bf16[1024,768]{1,0:T(8,128)(2,1)S(1)}, bf16[1024,768]{1,0:T(8,128)(2,1)}, u32[]{:S(2)}) copy-start(bf16[1024,768]{1,0:T(8,128)(2,1)} %param.15) | copy-start | bytes 4718596
  220.9 115.4 %copy-start.61 = (f32[768]{0:T(1024)}, f32[768]{0:T(1024)S(1)}, u32[]{:S(2)}) copy-start(f32[768]{0:T(1024)S(1)} %get-tuple-element.109) | copy-start | bytes 9220
  305.0 5.0 copy-start.28
  305.2 4.8 copy-start.30
  305.4 4.6 copy-start.83
  305.8 4.8 copy-start.27
  314.2 5.6 copy-start.2
  319.3 6.2 copy-start
  319.8 4.0 copy-start.64
  325.5 4.0 copy-start.56
  330.0 2.9 copy-start.58
  330.0 2.9 copy-start.20
  333.8 81.7 %copy-start.45 = (f32[1024]{0:T(1024)}, f32[1024]{0:T(1024)S(1)}, u32[]{:S(2)}) copy-start(f32[1024]{0:T(1024)S(1)} %broadcast_multiply_fusion.6) | copy-start | bytes 12292
  334.4 3.9 copy-start.52
  338.3 7.5 %copy-start.48 = (bf16[1024,8]{0,1:T(8,128)(2,1)}, bf16[1024,8]{0,1:T(8,128)(2,1)S(1)}, u32[]{:S(2)}) copy-start(bf16[1024,8]{0,1:T(8,128)(2,1)S(1)} %convolution_convert_fusion.6) | copy-start | bytes 49156
  345.9 9.9 %copy-start.47 = (bf16[3072,8]{0,1:T(8,128)(2,1)S(1)}, bf16[3072,8]{0,1:T(8,128)(2,1)}, u32[]{:S(2)}) copy-start(bf16[3072,8]{0,1:T(8,128)(2,1)} %reshape.756) | copy-start | bytes 147460
  357.5 8.9 %copy-start.50 = (bf16[1024,8]{0,1:T(8,128)(2,1)}, bf16[1024,8]{0,1:T(8,128)(2,1)S(1)}, u32[]{:S(2)}) copy-start(bf16[1024,8]{0,1:T(8,128)(2,1)S(1)} %convolution_convert_fusion.5) | copy-start | bytes 49156
  357.5 8.9 %copy-start.53 = (f32[1024]{0:T(1024)S(1)}, f32[1024]{0:T(1024)}, u32[]{:S(2)}) copy-start(f32[1024]{0:T(1024)} %copy-done.52) | copy-start | bytes 12292
  357.5 8.9 %copy-start.62 = (f32[768]{0:T(1024)S(1)}, f32[768]{0:T(1024)}, u32[]{:S(2)}) copy-start(f32[768]{0:T(1024)} %copy-done.61) | copy-start | bytes 9220
  357.5 8.9 %copy-start.69 = (f32[768]{0:T(1024)S(1)}, f32[768]{0:T(1024)}, u32[]{:S(2)}) copy-start(f32[768]{0:T(1024)} %get-tuple-element.111) | copy-start | bytes 9220
  367.4 3.5 copy-start.1
  367.9 3.0 copy-start.76
  370.0 3.5 slice-start.5
  373.5 8.0 %copy-start.18 = (bf16[1024,768]{0,1:T(8,128)(2,1)}, bf16[1024,768]{0,1:T(8,128)(2,1)S(1)}, u32[]{:S(2)}) copy-start(bf16[1024,768]{0,1:T(8,128)(2,1)S(1)} %get-tuple-element.118) | copy-start | bytes 4718596
  415.4 2.9 copy-start.70
  415.5 2.9 copy-start.72
  415.5 4.0 copy-start.80
  434.3 3.5 copy-start.14
  434.4 3.5 copy-start.42
  434.4 3.7 copy-start.31
  436.0 3.1 copy-start.29
  436.0 4.2 copy-start.12
  436.1 4.2 copy-start.55
  440.3 6.4 copy-start.3
  440.3 6.4 copy-start.22
  446.7 8.8 %slice-start = ((s8[12582912]{0:T(1024)(128)(4,1)}), s8[4194304]{0:T(1024)(128)(4,1)S(1)}, s32[]{:S(2)}) async-start(s8[12582912]{0:T(1024)(128)(4,1)} %bitcast.239), calls=%async_computation.5 | async-start | bytes 8388608
  448.1 7.4 %slice-start.1 = ((s8[12582912]{0:T(1024)(128)(4,1)}), s8[4194304]{0:T(1024)(128)(4,1)S(1)}, s32[]{:S(2)}) async-start(s8[12582912]{0:T(1024)(128)(4,1)} %bitcast.239), calls=%async_computation.6 | async-start | bytes 8388608
  450.0 5.5 slice-start.2
  450.7 4.8 copy-start.15
  450.7 4.8 copy-start.39
  479.8 10.7 %copy-start.33 = (bf16[128,12,64]{0,2,1:T(8,128)(2,1)S(1)}, bf16[128,12,64]{0,2,1:T(8,128)(2,1)}, u32[]{:S(2)}) copy-start(bf16[128,12,64]{0,2,1:T(8,128)(2,1)} %fusion.66) | copy-start | bytes 589828
  493.0 7.7 %slice-start.3 = ((s8[6291456]{0:T(1024)(128)(4,1)}), s8[2097152]{0:T(1024)(128)(4,1)S(1)}, s32[]{:S(2)}) async-start(s8[6291456]{0:T(1024)(128)(4,1)} %bitcast.257), calls=%async_computation.8 | async-start | bytes 4194304
  493.6 6.0 copy-start.7
  493.6 5.0 copy-start.41
  493.6 7.1 %slice-start.4 = ((s8[6291456]{0:T(1024)(128)(4,1)}), s8[4194304]{0:T(1024)(128)(4,1)S(1)}, s32[]{:S(2)}) async-start(s8[6291456]{0:T(1024)(128)(4,1)} %bitcast.257), calls=%async_computation.9 | async-start | bytes 8388608
  503.4 6.9 %copy-start.4 = (f32[1024,768]{0,1:T(8,128)S(1)}, f32[1024,768]{0,1:T(8,128)}, u32[]{:S(2)}) copy-start(f32[1024,768]{0,1:T(8,128)} %get-tuple-element.139) | copy-start | bytes 9437188
  503.4 6.9 %copy-start.46 = (f32[1024]{0:T(1024)S(1)}, f32[1024]{0:T(1024)}, u32[]{:S(2)}) copy-start(f32[1024]{0:T(1024)} %copy-done.45) | copy-start | bytes 12292
  503.4 6.9 %copy-start.54 = (f32[1024]{0:T(1024)S(1)}, f32[1024]{0:T(1024)}, u32[]{:S(2)}) copy-start(f32[1024]{0:T(1024)} %copy-done.52) | copy-start | bytes 12292
  503.4 6.9 %copy-start.71 = (f32[1024]{0:T(1024)S(1)}, f32[1024]{0:T(1024)}, u32[]{:S(2)}) copy-start(f32[1024]{0:T(1024)} %copy-done.70) | copy-start | bytes 12292
  503.4 6.9 %copy-start.73 = (f32[1024]{0:T(1024)S(1)}, f32[1024]{0:T(1024)}, u32[]{:S(2)}) copy-start(f32[1024]{0:T(1024)} %copy-done.72) | copy-start | bytes 12292
  512.7 130.3 %copy-start.32 = (f32[8,6912]{1,0:T(8,128)S(1)}, f32[8,6912]{1,0:T(8,128)}, u32[]{:S(2)}) copy-start(f32[8,6912]{1,0:T(8,128)} %param.25) | copy-start | bytes 663556
  512.7 130.3 %copy-start.43 = (f32[8,6912]{1,0:T(8,128)S(1)}, f32[8,6912]{1,0:T(8,128)}, u32[]{:S(2)}) copy-start(f32[8,6912]{1,0:T(8,128)} %param.27) | copy-start | bytes 663556
  512.7 130.4 %copy-start.44 = (f32[8,6912]{1,0:T(8,128)S(1)}, f32[8,6912]{1,0:T(8,128)}, u32[]{:S(2)}) copy-start(f32[8,6912]{1,0:T(8,128)} %param.26) | copy-start | bytes 663556
  (32 other events, 60.1 us)
Sparse Core Ops, SparseCore 0:
  11.4 60.8 all-gather.7
  75.2 52.5 all-gather.9
  131.3 63.4 all-gather.11
  198.1 62.1 all-gather.13
  503.5 137.1 all-reduce.1
where the time goes:
time: 659 us; the launch traced here: 655 us
  blocking collectives  251 us (38%)
  matrix products  168 us (25%)
  waiting for transfers between devices  124 us (19%)
  local copies, waits for them, and re-layouts  54 us (8%)
  other arithmetic  41 us (6%)
  between operations  17.3 us (3%)
    psum x1, waiting for transfers between devices, on_device(): b_grad = lax.psum(local_gradient, ('dp', 'fsdp'))  124 us
    all_gather x1, blocking collectives, on_device(): lax.all_gather(ln_gains.astype(brain_float_type), ('dp', 'fsdp'), axis=1,...  66 us
    all_gather x1, blocking collectives, on_device(): lax.all_gather(ln_biases.astype(brain_float_type), ('dp', 'fsdp'), axis=1...  64 us
    all_gather x1, blocking collectives, on_device(): lax.all_gather(a_down.astype(brain_float_type), ('dp', 'fsdp'), axis=0, t...  63.5 us
    dot_general x11, matrix products, transposed_product(): lax.dot_general(left, right, (((1,), (1,)), ((), ())), preferred_element_...  63.5 us
    all_gather x1, blocking collectives, on_device(): lax.all_gather(a_in.astype(brain_float_type), ('dp', 'fsdp'), axis=0, til...  57.2 us
    dot_general x14, matrix products, product_result(): return jnp.dot(left, right, preferred_element_type=jnp.float32)  47 us
    unnamed x188, local copies, waits for them, and re-layouts  22.4 us
  transfers between devices with their start and end apart: 5, of which 1 were waited for; matrix products, arithmetic and copies ran while one was open for 16% of the time, Pallas kernels for 0%

commit v1 on v0

--- a/solution.py
+++ b/solution.py
@@ -376,7 +376,7 @@
         ],
         axis=1,
     )
-    b_grad = lax.psum(local_gradient, ("dp", "fsdp"))
+    b_grad = jnp.sum(lax.all_gather(local_gradient, ("dp", "fsdp")), axis=0)
     grad_norm = jnp.sqrt(jnp.sum(b_grad * b_grad))
     moment_new, second_new, adapter_new = adam_update(
         b_grad, grad_norm, moment_one, moment_two, adapter_b

time: 659 us -> 603 us (0.915)
  waiting for transfers between devices: 124 us -> 63.7 us
    psum x1 -> x0, waiting for transfers between devices: 124 us -> none  [on_device(): b_grad = lax.psum(local_gradient, ('dp', 'fsdp'))]
    all_gather x0 -> x1, waiting for transfers between devices: none -> 63.6 us  [on_device(): b_grad = jnp.sum(lax.all_gather(local_gradient, ('dp', 'fsdp')), axis=0)]
    unnamed x188 -> x189, local copies, waits for them, and re-layouts: 22.4 us -> 24 us
  transfers between devices with their start and end apart: 5 -> 5, of which waited for: 1 -> 1; matrix products, arithmetic and copies ran while one was open for 16% -> 18% of each run, Pallas kernels for 0% -> 0%
where the time goes in v1:
time: 603 us; the launch traced here: 597 us
  blocking collectives  251 us (42%)
  matrix products  167 us (28%)
  waiting for transfers between devices  63.7 us (11%)
  local copies, waits for them, and re-layouts  55.6 us (9%)
  other arithmetic  42.5 us (7%)
  between operations  17.1 us (3%)
    all_gather x1, blocking collectives, on_device(): lax.all_gather(ln_gains.astype(brain_float_type), ('dp', 'fsdp'), axis=1,...  66.2 us
    all_gather x1, blocking collectives, on_device(): lax.all_gather(ln_biases.astype(brain_float_type), ('dp', 'fsdp'), axis=1...  63.8 us
    all_gather x1, waiting for transfers between devices, on_device(): b_grad = jnp.sum(lax.all_gather(local_gradient, ('dp', 'fsdp')), axis=0)  63.6 us
    all_gather x1, blocking collectives, on_device(): lax.all_gather(a_down.astype(brain_float_type), ('dp', 'fsdp'), axis=0, t...  63.5 us
    dot_general x11, matrix products, transposed_product(): lax.dot_general(left, right, (((1,), (1,)), ((), ())), preferred_element_...  63.1 us
    all_gather x1, blocking collectives, on_device(): lax.all_gather(a_in.astype(brain_float_type), ('dp', 'fsdp'), axis=0, til...  57.2 us
    dot_general x14, matrix products, product_result(): return jnp.dot(left, right, preferred_element_type=jnp.float32)  46.7 us
    unnamed x189, local copies, waits for them, and re-layouts  24 us
  transfers between devices with their start and end apart: 5, of which 1 were waited for; matrix products, arithmetic and copies ran while one was open for 18% of the time, Pallas kernels for 0%

profile of v1, /device:TPU:8, one launch (start us, length us, event | category | flops | bytes accessed | tf_op | source)
XLA Modules:
  0.0 597.0 jit_solution(18318769336345957307)
XLA Ops:
  7.2 1.7 convert_element_type.392
  10.6 1.6 convert_element_type.423
  12.3 1.6 convert_element_type.426
  22.8 57.2 %all_gather.36 = bf16[768,40]{1,0:T(8,128)(2,1)S(1)} all-gather(bf16[24,40]{1,0:T(8,128)(2,1)S(1)} %convert_element_type.393), channel_id=1, replica_groups=mesh['dp'=8,'fsdp'=4] {'dp','fsdp'}, dimensions={0}, use_global_device_ids=true | all-gather | bytes 63360 | tf_op jit(solution)/shard_map/all_gather | solution.py:215
  82.1 2.3 fusion.131
  84.4 2.4 fusion.134
  86.8 2.2 fusion.137
  89.9 63.8 %all-gather.1 = bf16[32,24,2]{1,2,0:T(2,128)(2,1)S(1)} all-gather(bf16[1,24,2]{1,2,0:T(2,128)(2,1)S(1)} %convert_bitcast_fusion.1), channel_id=1, replica_groups=mesh['dp'=8,'fsdp'=4] {'dp','fsdp'}, dimensions={0}, use_global_device_ids=true | all-gather | bytes 3168 | tf_op jit(solution)/shard_map/all_gather | solution.py:218
  153.7 66.2 %all-gather = bf16[32,24,2]{1,2,0:T(2,128)(2,1)S(1)} all-gather(bf16[1,24,2]{1,2,0:T(2,128)(2,1)S(1)} %convert_bitcast_fusion.2), channel_id=1, replica_groups=mesh['dp'=8,'fsdp'=4] {'dp','fsdp'}, dimensions={0}, use_global_device_ids=true | all-gather | bytes 3168 | tf_op jit(solution)/shard_map/all_gather | solution.py:217
  221.6 63.5 %all-gather.2 = bf16[32,96,8]{1,2,0:T(8,128)(2,1)S(1)} all-gather(bf16[1,96,8]{1,2,0:T(8,128)(2,1)S(1)} %convert_bitcast_fusion), channel_id=1, replica_groups=mesh['dp'=8,'fsdp'=4] {'dp','fsdp'}, dimensions={0}, use_global_device_ids=true | all-gather | bytes 50688 | tf_op jit(solution)/shard_map/all_gather | solution.py:216
  288.2 8.8 %fusion.9 = bf16[1024,2304]{1,0:T(8,128)(2,1)} fusion(f32[1024,768]{1,0:T(8,128)} %fusion.131, f32[1024,768]{1,0:T(8,128)} %fusion.134, f32[1024,768]{1,0:T(8,128)} %fusion.137, bf16[1024,768]{1,0:T(8,128)(2,1)S(1)} %copy-done.18, bf16[768,2304]{1,0:T(8,128)(2,1)} %all-gather.9.cloned.1.call-done), kind=kOutput, calls=%fused_computation.20 | convolution fusion | flops 3635675136 | bytes 19267584 | tf_op jit(solution)/shard_map/dot_general | solution.py:38
  297.0 6.6 %copy.153 = bf16[1024,2304]{0,1:T(8,128)(2,1)} copy(bf16[1024,2304]{1,0:T(8,128)(2,1)} %fusion.9) | data formatting | bytes 9437184 | tf_op jit(solution)/shard_map/convert_element_type | solution.py:256
  312.3 1.9 fusion.168
  314.2 5.1 fusion.169
  319.8 2.0 fusion.48
  321.8 2.0 copy-done.65
  323.8 1.8 fusion.6
  325.6 4.1 fusion.26
  330.1 2.8 fusion.111
  338.5 7.5 %fusion.174 = f32[1024,3072]{1,0:T(8,128)S(1)} fusion(bf16[1024,768]{0,1:T(8,128)(2,1)} %copy-done.9, bf16[768,3072]{1,0:T(8,128)(2,1)} %all-gather.13.cloned.1.call-done), kind=kOutput, calls=%fused_computation.259 | convolution fusion | flops 4831838208 | bytes 18874368 | tf_op jit(solution)/shard_map/dot_general | solution.py:38
  346.0 6.9 %multiply_convert_fusion.1 = (bf16[1024,3072]{1,0:T(8,128)(2,1)S(1)}, f32[1024,3072]{1,0:T(8,128)}) fusion(f32[1024,3072]{1,0:T(8,128)S(1)} %fusion.174, bf16[1024,8]{0,1:T(8,128)(2,1)S(1)} %convolution_convert_fusion.6, bf16[8,6912]{1,0:T(8,128)(2,1)S(1)} %convert_element_type.395), kind=kOutput, calls=%fused_computation.10 | convolution fusion | flops 72351744 | bytes 31522816 | tf_op jit(solution)/shard_map/dot_general | solution.py:38
  352.9 2.7 copy-done.6
  355.6 1.7 convolution_convert_fusion.5
  357.3 8.8 %fusion.175 = f32[1024,768]{0,1:T(8,128)S(1)} fusion(bf16[1024,3072]{1,0:T(8,128)(2,1)} %copy-done.6, bf16[3072,768]{1,0:T(8,128)(2,1)} %all-gather.15.cloned.1.call-done), kind=kOutput, calls=%fused_computation.260 | convolution fusion | flops 4831838208 | bytes 14155776 | tf_op jit(solution)/shard_map/dot_general | solution.py:38
  367.7 2.1 copy-done.5
  370.7 2.6 fusion.120
  373.4 8.1 %fusion.176 = f32[1024,3072]{1,0:T(8,128)} fusion(bf16[1024,768]{0,1:T(8,128)(2,1)S(1)} %get-tuple-element.118, bf16[3072,768]{1,0:T(8,128)(2,1)S(1)} %bitcast.304), kind=kOutput, calls=%fused_computation.261 | convolution fusion | flops 4831838208 | bytes 18874368 | tf_op jit(solution)/shard_map/dot_general | solution.py:42
  381.4 13.7 %fusion.5 = bf16[1024,3072]{1,0:T(8,128)(2,1)} fusion(f32[1024,3072]{1,0:T(8,128)} %get-tuple-element.136, f32[1024,3072]{1,0:T(8,128)} %fusion.176, bf16[3072,8]{0,1:T(8,128)(2,1)S(1)} %copy-done.48, bf16[1024,768]{0,1:T(8,128)(2,1)} %copy-done.19, bf16[8,6912]{1,0:T(8,128)(2,1)S(1)} %convert_element_type.395), kind=kOutput, calls=%fused_computation.6 | convolution fusion | flops 97533952 | bytes 33091584 | tf_op jit(solution)/shard_map/dot_general | solution.py:42
  395.1 10.0 %fusion.177 = f32[1024,768]{0,1:T(8,128)} fusion(bf16[1024,3072]{1,0:T(8,128)(2,1)} %fusion.5, bf16[768,3072]{1,0:T(8,128)(2,1)} %all-gather.13.cloned.1.call-done), kind=kOutput, calls=%fused_computation.262 | convolution fusion | flops 4831838208 | bytes 14155776 | tf_op jit(solution)/shard_map/dot_general | solution.py:42
  405.1 10.2 %fusion.161 = (f32[1024]{0:T(1024)S(1)}, f32[1024]{0:T(1024)S(1)}, f32[1024,768]{0,1:T(8,128)}) fusion(f32[1024]{0:T(1024)S(1)} %copy-done.54, f32[1024,768]{0,1:T(8,128)S(1)} %get-tuple-element.134, f32[1024]{0:T(1024)S(1)} %broadcast_multiply_fusion.6, f32[768]{0:T(1024)S(1)} %copy-done.63, bf16[768,40]{1,0:T(8,128)(2,1)S(1)} %all_gather.36, ...), kind=kOutput, calls=%fused_computation.249 | convolution fusion | flops 76298240 | bytes 20738048 | tf_op jit(solution)/shard_map/dot_general | solution.py:42
  415.4 2.8 fusion.96
  419.4 3.0 fusion.178
  422.4 4.4 add_convert_fusion.1
  426.8 1.8 slice.306
  428.6 1.7 fusion.164
  430.3 2.1 slice.305
  432.4 1.9 reshape.820
  434.2 1.7 fusion.55
  436.0 1.7 multiply_reduce_fusion.6
  442.7 2.0 fusion.65
  444.7 1.8 fusion.66
  447.9 1.9 multiply_reduce_fusion.1
  450.6 2.6 fusion.56
  453.2 2.2 fusion.57
  455.4 3.3 fusion.39
  458.7 7.2 %multiply_reduce_fusion = (f32[12,512]{1,0:T(8,128)S(1)}, f32[12,512,512]{1,2,0:T(8,128)}) fusion(f32[12,512,512]{1,2,0:T(8,128)S(1)} %bitcast.264, f32[12,512]{1,0:T(8,128)S(1)} %copy-done.40, bf16[512,12,64]{0,2,1:T(8,128)(2,1)S(1)} %bitcast.291, bf16[1,1024,3,12,64]{1,4,3,2,0:T(8,128)(2,1)} %bitcast.278), kind=kOutput, calls=%fused_computation.8 | convolution fusion | flops 412084224 | bytes 26787840 | tf_op jit(solution)/shard_map/while/body/eval_jaxpr/gqhe,gkhe->ghqk/dot_general | solution.py:102
  465.8 6.8 %multiply_convert_fusion = bf16[12,512,512]{1,2,0:T(8,128)(2,1)S(1)} fusion(f32[12,512,512]{1,2,0:T(8,128)} %get-tuple-element.147, f32[12,512,512]{1,2,0:T(8,128)S(1)} %bitcast.264, f32[12,512]{1,0:T(8,128)S(1)} %get-tuple-element.146, f32[12,512]{1,0:T(8,128)S(1)} %copy-done.40), kind=kLoop, calls=%fused_computation.7 | loop fusion | flops 12582912 | bytes 31506432 | tf_op jit(solution)/shard_map/while/body/eval_jaxpr/convert_element_type | solution.py:106
  472.6 4.0 fusion.44
  476.7 3.2 fusion.43
  481.0 1.9 reshape.829
  482.9 1.9 copy.176
  484.8 1.9 reshape.821
  486.7 1.9 copy.183
  488.6 1.9 reshape.825
  490.6 1.7 maximum_bitcast_fusion.2
  500.6 2.7 copy.192
  503.4 1.9 fusion.29
  505.2 1.7 fusion.33
  507.0 1.7 fusion.37
  508.8 6.0 %fusion.179 = f32[1024,768]{0,1:T(8,128)S(1)} fusion(bf16[768,2304]{1,0:T(8,128)(2,1)} %all-gather.9.cloned.1.call-done, bf16[1024,2304]{0,1:T(8,128)(2,1)S(1)} %bitcast.289), kind=kOutput, calls=%fused_computation.264 | convolution fusion | flops 3623878656 | bytes 11403264 | tf_op jit(solution)/shard_map/dot_general | solution.py:42
  514.8 2.4 add_convert_fusion
  517.2 2.6 copy.193
  519.8 63.6 %all-gather.17.cloned.1.call-done = f32[32,8,6912]{2,1,0:T(8,128)} async-done(((f32[1,8,6912]{2,1,0:T(8,128)}), f32[32,8,6912]{2,1,0:T(8,128)}) %all-gather.17.cloned.1.call-update) | async-done | bytes 7077904 | tf_op jit(solution)/shard_map/all_gather | solution.py:379
  583.4 3.3 reduce_sum.186
  (286 shorter events, 54.6 us)
Async XLA Ops:
  7.2 72.8 %copy-start.18 = (bf16[1024,768]{1,0:T(8,128)(2,1)S(1)}, bf16[1024,768]{1,0:T(8,128)(2,1)}, u32[]{:S(2)}) copy-start(bf16[1024,768]{1,0:T(8,128)(2,1)} %param.14) | copy-start | bytes 4718596
  7.2 281.0 %all-gather.9.cloned.1.call-start = ((), (), s32[]{:S(2)}) async-start(), calls=%async_computation | async-start | bytes 3649536 | tf_op jit(solution)/shard_map/all_gather | solution.py:209
  8.9 321.2 %all-gather.11.cloned.1.call-start = ((), (), s32[]{:S(2)}) async-start(), calls=%async_computation.1 | async-start | bytes 1216512 | tf_op jit(solution)/shard_map/all_gather | solution.py:212
  10.5 328.0 %all-gather.13.cloned.1.call-start = ((), (), s32[]{:S(2)}) async-start(), calls=%async_computation.2 | async-start | bytes 4866048 | tf_op jit(solution)/shard_map/all_gather | solution.py:213
  12.2 345.1 %all-gather.15.cloned.1.call-start = ((), (), s32[]{:S(2)}) async-start(), calls=%async_computation.3 | async-start | bytes 4866048 | tf_op jit(solution)/shard_map/all_gather | solution.py:214
  14.0 569.4 %all-gather.17.cloned.1.call-start = ((), (), s32[]{:S(2)}) async-start(), calls=%async_computation.4 | async-start | bytes 7299072 | tf_op jit(solution)/shard_map/all_gather | solution.py:379
  22.8 399.6 %copy-start.39 = (bf16[8,6912]{1,0:T(8,128)(2,1)}, bf16[8,6912]{1,0:T(8,128)(2,1)S(1)}, u32[]{:S(2)}) copy-start(bf16[8,6912]{1,0:T(8,128)(2,1)S(1)} %convert_element_type.395) | copy-start | bytes 331780
  82.1 4.7 copy-start.41
  84.4 5.4 copy-start.82
  84.4 5.4 copy-start.83
  84.4 5.5 copy-start.78
  84.4 201.5 %copy-start.27 = (bf16[1024,768]{1,0:T(8,128)(2,1)S(1)}, bf16[1024,768]{1,0:T(8,128)(2,1)}, u32[]{:S(2)}) copy-start(bf16[1024,768]{1,0:T(8,128)(2,1)} %param.15) | copy-start | bytes 4718596
  220.8 115.6 %copy-start.62 = (f32[768]{0:T(1024)}, f32[768]{0:T(1024)S(1)}, u32[]{:S(2)}) copy-start(f32[768]{0:T(1024)S(1)} %get-tuple-element.109) | copy-start | bytes 9220
  305.0 5.0 copy-start.29
  305.2 4.8 copy-start.31
  305.4 4.6 copy-start.84
  305.8 4.8 copy-start.28
  314.2 5.6 copy-start.2
  319.3 6.2 %copy-start = (f32[12,512,512]{1,2,0:T(8,128)}, f32[12,512,512]{1,2,0:T(8,128)S(1)}, u32[]{:S(2)}) copy-start(f32[12,512,512]{1,2,0:T(8,128)S(1)} %get-tuple-element.132) | copy-start | bytes 37748740
  319.8 4.0 copy-start.65
  325.5 4.2 copy-start.57
  330.1 2.9 copy-start.21
  333.9 81.5 %copy-start.46 = (f32[1024]{0:T(1024)}, f32[1024]{0:T(1024)S(1)}, u32[]{:S(2)}) copy-start(f32[1024]{0:T(1024)S(1)} %broadcast_multiply_fusion.6) | copy-start | bytes 12292
  334.5 3.9 copy-start.53
  338.5 7.5 %copy-start.49 = (bf16[1024,8]{0,1:T(8,128)(2,1)}, bf16[1024,8]{0,1:T(8,128)(2,1)S(1)}, u32[]{:S(2)}) copy-start(bf16[1024,8]{0,1:T(8,128)(2,1)S(1)} %convolution_convert_fusion.6) | copy-start | bytes 49156
  346.0 9.6 %copy-start.48 = (bf16[3072,8]{0,1:T(8,128)(2,1)S(1)}, bf16[3072,8]{0,1:T(8,128)(2,1)}, u32[]{:S(2)}) copy-start(bf16[3072,8]{0,1:T(8,128)(2,1)} %reshape.837) | copy-start | bytes 147460
  357.3 8.9 %copy-start.51 = (bf16[1024,8]{0,1:T(8,128)(2,1)}, bf16[1024,8]{0,1:T(8,128)(2,1)S(1)}, u32[]{:S(2)}) copy-start(bf16[1024,8]{0,1:T(8,128)(2,1)S(1)} %convolution_convert_fusion.5) | copy-start | bytes 49156
  357.3 8.9 %copy-start.54 = (f32[1024]{0:T(1024)S(1)}, f32[1024]{0:T(1024)}, u32[]{:S(2)}) copy-start(f32[1024]{0:T(1024)} %copy-done.53) | copy-start | bytes 12292
  357.3 8.9 %copy-start.63 = (f32[768]{0:T(1024)S(1)}, f32[768]{0:T(1024)}, u32[]{:S(2)}) copy-start(f32[768]{0:T(1024)} %copy-done.62) | copy-start | bytes 9220
  357.3 8.9 %copy-start.70 = (f32[768]{0:T(1024)S(1)}, f32[768]{0:T(1024)}, u32[]{:S(2)}) copy-start(f32[768]{0:T(1024)} %get-tuple-element.111) | copy-start | bytes 9220
  367.3 3.5 copy-start.1
  367.7 3.0 copy-start.77
  369.8 3.5 slice-start.5
  373.3 8.1 %copy-start.19 = (bf16[1024,768]{0,1:T(8,128)(2,1)}, bf16[1024,768]{0,1:T(8,128)(2,1)S(1)}, u32[]{:S(2)}) copy-start(bf16[1024,768]{0,1:T(8,128)(2,1)S(1)} %get-tuple-element.118) | copy-start | bytes 4718596
  415.4 4.0 copy-start.81
  434.2 3.5 copy-start.15
  434.2 3.5 copy-start.43
  434.2 3.7 copy-start.32
  435.9 3.1 copy-start.30
  435.9 4.2 copy-start.13
  435.9 4.2 copy-start.56
  440.2 6.4 %copy-start.3 = (f32[12,256,256]{1,2,0:T(8,128)S(1)}, f32[12,256,256]{1,2,0:T(8,128)}, u32[]{:S(2)}) copy-start(f32[12,256,256]{1,2,0:T(8,128)} %copy-done.2) | copy-start | bytes 9437188
  440.2 6.4 %copy-start.22 = (bf16[256,768]{0,1:T(8,128)(2,1)S(1)}, bf16[256,768]{0,1:T(8,128)(2,1)}, u32[]{:S(2)}) copy-start(bf16[256,768]{0,1:T(8,128)(2,1)} %slice.306) | copy-start | bytes 1179652
  446.6 8.8 %slice-start = ((s8[12582912]{0:T(1024)(128)(4,1)}), s8[4194304]{0:T(1024)(128)(4,1)S(1)}, s32[]{:S(2)}) async-start(s8[12582912]{0:T(1024)(128)(4,1)} %bitcast.263), calls=%async_computation.5 | async-start | bytes 8388608
  447.9 7.4 %slice-start.1 = ((s8[12582912]{0:T(1024)(128)(4,1)}), s8[4194304]{0:T(1024)(128)(4,1)S(1)}, s32[]{:S(2)}) async-start(s8[12582912]{0:T(1024)(128)(4,1)} %bitcast.263), calls=%async_computation.6 | async-start | bytes 8388608
  449.9 5.4 slice-start.2
  450.5 4.8 copy-start.16
  450.6 4.8 copy-start.40
  479.8 10.7 %copy-start.34 = (bf16[128,12,64]{0,2,1:T(8,128)(2,1)S(1)}, bf16[128,12,64]{0,2,1:T(8,128)(2,1)}, u32[]{:S(2)}) copy-start(bf16[128,12,64]{0,2,1:T(8,128)(2,1)} %fusion.67) | copy-start | bytes 589828
  492.8 4.8 slice-start.3
  493.0 4.9 slice-start.4
  493.6 4.0 copy-start.7
  493.6 3.5 copy-start.11
  493.6 3.5 copy-start.60
  494.0 4.0 copy-start.50
  503.4 5.4 copy-start.8
  508.7 6.0 %copy-start.4 = (f32[1024,768]{0,1:T(8,128)S(1)}, f32[1024,768]{0,1:T(8,128)}, u32[]{:S(2)}) copy-start(f32[1024,768]{0,1:T(8,128)} %get-tuple-element.139) | copy-start | bytes 9437188
  508.7 6.0 %copy-start.47 = (f32[1024]{0:T(1024)S(1)}, f32[1024]{0:T(1024)}, u32[]{:S(2)}) copy-start(f32[1024]{0:T(1024)} %copy-done.46) | copy-start | bytes 12292
  508.7 6.0 %copy-start.55 = (f32[1024]{0:T(1024)S(1)}, f32[1024]{0:T(1024)}, u32[]{:S(2)}) copy-start(f32[1024]{0:T(1024)} %copy-done.53) | copy-start | bytes 12292
  508.7 6.0 %copy-start.72 = (f32[1024]{0:T(1024)S(1)}, f32[1024]{0:T(1024)}, u32[]{:S(2)}) copy-start(f32[1024]{0:T(1024)} %copy-done.71) | copy-start | bytes 12292
  508.7 6.0 %copy-start.74 = (f32[1024]{0:T(1024)S(1)}, f32[1024]{0:T(1024)}, u32[]{:S(2)}) copy-start(f32[1024]{0:T(1024)} %copy-done.73) | copy-start | bytes 12292
  519.8 68.4 %copy-start.33 = (f32[8,6912]{1,0:T(8,128)S(1)}, f32[8,6912]{1,0:T(8,128)}, u32[]{:S(2)}) copy-start(f32[8,6912]{1,0:T(8,128)} %param.25) | copy-start | bytes 663556
  519.8 68.4 %copy-start.44 = (f32[8,6912]{1,0:T(8,128)S(1)}, f32[8,6912]{1,0:T(8,128)}, u32[]{:S(2)}) copy-start(f32[8,6912]{1,0:T(8,128)} %param.27) | copy-start | bytes 663556
  519.8 68.4 %copy-start.45 = (f32[8,6912]{1,0:T(8,128)S(1)}, f32[8,6912]{1,0:T(8,128)}, u32[]{:S(2)}) copy-start(f32[8,6912]{1,0:T(8,128)} %param.26) | copy-start | bytes 663556
  (33 other events, 61.7 us)
Sparse Core Ops, SparseCore 0:
  11.4 60.8 all-gather.8
  75.3 52.5 all-gather.10
  131.3 63.4 all-gather.12
  198.1 62.0 all-gather.14
  500.7 82.6 all-gather.16
